TPU v7x, 32 devices: a whole 2x2x4 slice. The times are simulated.
32 devices in a mesh: batch: 8 (over z, y), vocab: 4 (over x, core).
Axes of the slice: x: 2, y: 2, z: 4, core: 2. Of those that a mesh axis runs over, the one named last changes fastest.
Arguments:
- hidden: bfloat16 [4096, 3584], P(('batch', 'vocab')), may hold values from -6 to 6
- head_weight: bfloat16 [3072, 3584], P('vocab', 'batch'), may hold values from -0.3125 to 0.3125
- targets: int32 [4096], P(('batch', 'vocab')), may hold values from 0 to 3071
- valid_mask: int32 [4096], P(('batch', 'vocab')), may hold values 0 or 1
Outputs:
- head_grad: float32 [3072, 3584], P('vocab', 'batch')
- hidden_grad: float32 [4096, 3584], P(('batch', 'vocab'))
- mean_loss: float32 [], replicated
All inputs are finite; a program needn't handle non-finite values. No bound on the sum of `valid_mask` on one device may be relied on, other than what follows from the above.
Results may differ from a plain program's by a relative error of at most 0.0019.
Values may be sent and summed in bfloat16 or wider, within the bound.
A program may use at most 128 MiB of HBM per device.

v0:
```python
import jax
import jax.numpy as jnp
from jax import lax
from jax.sharding import PartitionSpec as P

softcap = 30.0


def capped(scores):
    return softcap * jnp.tanh(scores / softcap)


def local(hidden, head_weight, targets, valid_mask):
    own_rows = head_weight.shape[0]
    batch_count = lax.axis_size("batch")
    vocab_index = lax.axis_index("vocab")
    group_ids, group_mask = (
        lax.all_gather(targets, "vocab", axis=0, tiled=True),
        lax.all_gather(valid_mask, "vocab", axis=0, tiled=True),
    )
    group_states = lax.all_gather(hidden, "vocab", axis=0, tiled=True)
    group_tokens = group_states.shape[0]
    first_row = vocab_index * own_rows
    inside = (group_ids >= first_row) & (group_ids < first_row + own_rows)
    local_index = jnp.where(inside, group_ids - first_row, -1)
    columns = jnp.arange(own_rows, dtype=jnp.int32)
    weight = group_mask.astype(jnp.float32)
    state_cols = group_states
    scores = lax.dot_general(
        state_cols,
        lax.all_gather(head_weight, "batch", axis=1, tiled=True),
        (((1,), (1,)), ((), ())),
        preferred_element_type=jnp.float32,
    )
    logits = capped(scores)
    target_hit = columns[None, :] == local_index[:, None]
    exponent = jnp.exp(logits)
    partition, target_logit = lax.psum(
        (jnp.sum(exponent, axis=1), jnp.sum(jnp.where(target_hit, logits, 0.0), axis=1)), "vocab"
    )
    slope = 1.0 - (logits / softcap) ** 2
    delta_logit = (
        weight[:, None] * (exponent / partition[:, None] - target_hit.astype(jnp.float32)) * slope
    ).astype(jnp.bfloat16)
    state_cols = group_states
    grad_columns = lax.psum_scatter(
        lax.dot_general(
            state_cols, delta_logit, (((0,), (0,)), ((), ())), preferred_element_type=jnp.float32
        ),
        "batch",
        scatter_dimension=0,
        tiled=True,
    )
    head_grad = jnp.transpose(grad_columns)
    partial_grad = jnp.dot(
        delta_logit,
        lax.all_gather(head_weight, "batch", axis=1, tiled=True),
        preferred_element_type=jnp.float32,
    )
    hidden_grad = lax.psum_scatter(partial_grad, "vocab", scatter_dimension=0, tiled=True)
    token_loss = weight * (jnp.log(partition) - target_logit)
    total_tokens = group_tokens * batch_count
    loss_total = lax.psum(jnp.sum(token_loss), "batch")
    mean_loss = loss_total / total_tokens
    return (head_grad, hidden_grad, mean_loss)


def solution(mesh):
    placed = (
        P(("batch", "vocab"), None),
        P("vocab", "batch"),
        P(("batch", "vocab")),
        P(("batch", "vocab")),
    )
    return jax.shard_map(
        local,
        mesh=mesh,
        in_specs=placed,
        out_specs=(P("vocab", "batch"), P(("batch", "vocab"), None), P()),
        check_vma=False,
    )
```

profile of v0, /device:TPU:0, one launch (start us, length us, event | category | flops | bytes accessed | tf_op | source)
XLA Modules:
  0.0 417.8 jit_solution(7849890568541200374)
XLA Ops:
  7.2 0.0 copy-start
  7.2 0.0 copy-start.1
  7.2 0.0 all-gather.5.cloned.1.call-start
  7.2 0.7 all-gather.5.cloned.1.call-update
  7.9 0.0 all-gather.7.cloned.1.call-start
  8.0 0.7 all-gather.7.cloned.1.call-update
  8.7 0.0 reduce-scatter.5.cloned.1.call-start
  8.7 0.0 copy-done
  8.7 6.0 %all-gather = s32[4,1,128]{2,1,0:T(1,128)S(1)} all-gather(s32[1,1,128]{2,1,0:T(1,128)S(1)} %bitcast.19), channel_id=1, replica_groups=mesh['batch'=8,'vocab'=4] {'vocab'}, dimensions={0}, use_global_device_ids=true | all-gather | bytes 2560 | tf_op jit(solution)/shard_map/all_gather | solution.py:19
  14.7 0.0 copy-done.1
  14.7 5.4 %all-gather.1 = s32[4,1,128]{2,1,0:T(1,128)S(1)} all-gather(s32[1,1,128]{2,1,0:T(1,128)S(1)} %bitcast.20), channel_id=1, replica_groups=mesh['batch'=8,'vocab'=4] {'vocab'}, dimensions={0}, use_global_device_ids=true | all-gather | bytes 2560 | tf_op jit(solution)/shard_map/all_gather | solution.py:18
  20.1 23.7 %all-gather.5.cloned.1.call-done = bf16[512,3584]{1,0:T(8,128)(2,1)} async-done(((bf16[128,3584]{1,0:T(8,128)(2,1)}), bf16[512,3584]{1,0:T(8,128)(2,1)}) %all-gather.5.cloned.1.call-update) | async-done | bytes 3670032 | tf_op jit(solution)/shard_map/all_gather | solution.py:21
  43.8 91.3 %all-gather.7.cloned.1.call-done = bf16[768,3584]{0,1:T(8,128)(2,1)} async-done(((bf16[768,448]{0,1:T(8,128)(2,1)}), bf16[768,3584]{0,1:T(8,128)(2,1)}) %all-gather.7.cloned.1.call-update) | async-done | bytes 5505040 | tf_op jit(solution)/shard_map/all_gather | solution.py:31
  135.1 7.0 %select_reduce_fusion = (f32[512]{0:T(512)S(1)}, f32[512]{0:T(512)S(1)}, f32[512,768]{1,0:T(8,128)S(1)}) fusion(s32[512]{0:T(512)S(1)} %bitcast.16, bf16[512,3584]{1,0:T(8,128)(2,1)} %all-gather.5.cloned.1.call-done, bf16[768,3584]{0,1:T(8,128)(2,1)} %all-gather.7.cloned.1.call-done), kind=kOutput, calls=%fused_computation.1 | convolution fusion | flops 2820930560 | bytes 10754048 | tf_op jit(solution)/shard_map/dot_general | solution.py:29
  142.1 5.7 %all-reduce = (f32[512]{0:T(512)S(1)}, f32[512]{0:T(512)S(1)}) all-reduce(f32[512]{0:T(512)S(1)} %get-tuple-element.10, f32[512]{0:T(512)S(1)} %get-tuple-element.9), channel_id=1, replica_groups=mesh['batch'=8,'vocab'=4] {'vocab'}, use_global_device_ids=true, to_apply=%region_1.2 | all-reduce | flops 1024 | bytes 8192 | tf_op jit(solution)/shard_map/psum | solution.py:38
  147.8 8.2 %fusion = f32[512,3584]{1,0:T(8,128)} fusion(bf16[768,3584]{0,1:T(8,128)(2,1)} %all-gather.7.cloned.1.call-done, f32[512,768]{1,0:T(8,128)S(1)} %get-tuple-element.13, s32[512]{0:T(512)S(1)} %bitcast.17, f32[512]{0:T(512)S(1)} %get-tuple-element.11, f32[512]{0:T(512)S(1)} %bitcast.13), kind=kOutput, calls=%fused_computation.8 | convolution fusion | flops 2822504448 | bytes 14424064 | tf_op jit(solution)/shard_map/dot_general | solution.py:55
  156.0 0.0 reduce-scatter.5.cloned.1.call-update
  156.0 0.0 reduce-scatter.7.cloned.1.call-start
  156.1 8.9 %convolution_bitcast_fusion = f32[3584,768]{0,1:T(8,128)} fusion(bf16[512,3584]{1,0:T(8,128)(2,1)} %all-gather.5.cloned.1.call-done, f32[512,768]{1,0:T(8,128)S(1)} %get-tuple-element.13, s32[512]{0:T(512)S(1)} %bitcast.18, f32[512]{0:T(512)S(1)} %get-tuple-element.11, f32[512]{0:T(512)S(1)} %bitcast.14), kind=kOutput, calls=%fused_computation | convolution fusion | flops 2822504448 | bytes 16259072 | tf_op jit(solution)/shard_map/dot_general | solution.py:47
  165.0 12.7 %copy.9 = f32[3584,768]{1,0:T(8,128)} copy(f32[3584,768]{0,1:T(8,128)} %convolution_bitcast_fusion) | data formatting | bytes 22020096
  177.7 0.0 reduce-scatter.7.cloned.1.call-update
  177.7 0.6 multiply_reduce_fusion
  178.3 19.4 %psum.23 = f32[]{:T(128)} all-reduce(f32[]{:T(128)} %multiply_reduce_fusion), channel_id=1, replica_groups=mesh['batch'=8,'vocab'=4] {'batch'}, use_global_device_ids=true, to_apply=%region_7.8 | all-reduce | flops 1 | bytes 8 | tf_op jit(solution)/shard_map/psum | solution.py:63
  198.4 22.1 %reduce-scatter.5.cloned.1.call-done = f32[128,3584]{1,0:T(8,128)} async-done(((f32[512,3584]{1,0:T(8,128)}), f32[128,3584]{1,0:T(8,128)}) %reduce-scatter.5.cloned.1.call-update) | async-done | bytes 1835024 | tf_op jit(solution)/shard_map/reduce_scatter | solution.py:60
  220.5 189.6 %reduce-scatter.7.cloned.1.call-done = f32[448,768]{1,0:T(8,128)} async-done(((f32[3584,768]{1,0:T(8,128)}), f32[448,768]{1,0:T(8,128)}) %reduce-scatter.7.cloned.1.call-update) | async-done | bytes 1376272
  (2 shorter events, 0.0 us)
Async XLA Ops:
  7.2 1.6 copy-start
  7.2 7.6 %copy-start.1 = (s32[128]{0:T(128)S(1)}, s32[128]{0:T(128)}, u32[]{:S(2)}) copy-start(s32[128]{0:T(128)} %param.6) | copy-start | bytes 1540
  7.2 36.6 %all-gather.5.cloned.1.call-start = ((), (), s32[]{:S(2)}) async-start(), calls=%async_computation.2 | async-start | bytes 4587520 | tf_op jit(solution)/shard_map/all_gather | solution.py:21
  7.9 127.2 %all-gather.7.cloned.1.call-start = ((), (), s32[]{:S(2)}) async-start(), calls=%async_computation.3 | async-start | bytes 6193152 | tf_op jit(solution)/shard_map/all_gather | solution.py:31
  8.7 211.9 %reduce-scatter.5.cloned.1.call-start = ((), (), s32[]{:S(2)}) async-start(), calls=%async_computation.4 | async-start | bytes 9175040 | tf_op jit(solution)/shard_map/reduce_scatter | solution.py:60
  156.0 254.1 %reduce-scatter.7.cloned.1.call-start = ((), (), s32[]{:S(2)}) async-start(), calls=%async_computation.5 | async-start | bytes 12386304
Sparse Core Ops, SparseCore 0:
  9.6 34.1 all-gather.4
  46.0 89.1 all-gather.6
  156.1 64.3 reduce-scatter.4
  224.6 185.4 reduce-scatter.6
where the time goes:
time: 418 us
  waiting for transfers between devices  328 us (78%)
  blocking collectives  36.5 us (9%)
  matrix products  24.1 us (6%)
  between operations  15.6 us (4%)
  local copies, waits for them, and re-layouts  12.7 us (3%)
    unnamed x5, waiting for transfers between devices  191 us
    all_gather x1, waiting for transfers between devices, local(): lax.all_gather(head_weight, 'batch', axis=1, tiled=True)  91.3 us
    all_gather x1, waiting for transfers between devices, local(): group_states = lax.all_gather(hidden, 'vocab', axis=0, tiled=True)  23.7 us
    reduce_scatter x1, waiting for transfers between devices, local(): lax.psum_scatter(partial_grad, 'vocab', scatter_dimension=0, tiled=True)  22.1 us
    psum x1, blocking collectives, local(): loss_total = lax.psum(jnp.sum(token_loss), 'batch')  19.4 us
    unnamed x5, local copies, waits for them, and re-layouts  12.7 us
    dot_general x1, matrix products, local(): lax.dot_general(state_cols, delta_logit, (((0,), (0,)), ((), ())), prefer...  8.94 us
  transfers between devices with their start and end apart: 4, of which 4 were waited for; matrix products, arithmetic and copies ran while one was open for 5% of the time, Pallas kernels for 0%

commit v1 on v0

--- a/solution.py
+++ b/solution.py
@@ -18,7 +18,14 @@
         lax.all_gather(targets, "vocab", axis=0, tiled=True),
         lax.all_gather(valid_mask, "vocab", axis=0, tiled=True),
     )
-    group_states = lax.all_gather(hidden, "vocab", axis=0, tiled=True)
+    ring = [hidden]
+    for hop in range(3):
+        ring.append(lax.ppermute(ring[-1], "vocab", [(dev, (dev + 1) % 4) for dev in range(4)]))
+    group_states = jnp.roll(
+        jnp.concatenate(ring[::-1], axis=0),
+        (lax.axis_index("vocab") + 1) * ring[0].shape[0],
+        axis=0,
+    )
     group_tokens = group_states.shape[0]
     first_row = vocab_index * own_rows
     inside = (group_ids >= first_row) & (group_ids < first_row + own_rows)

time: 418 us -> 386 us (0.923)
  waiting for transfers between devices: 328 us -> 289 us
  blocking collectives: 36.5 us -> 45.5 us
  local copies, waits for them, and re-layouts: 12.7 us -> 8.04 us
    unnamed x5 -> x3, waiting for transfers between devices: 191 us -> 0.71 us
    reduce_scatter x0 -> x1, waiting for transfers between devices: none -> 190 us  [local(): lax.psum_scatter(lax.dot_general(state_cols, delta_logit, (((0,), (0,)),...]
    all_gather x1, waiting for transfers between devices: 91.3 us -> 40.3 us  [local(): lax.all_gather(head_weight, 'batch', axis=1, tiled=True)]
    ppermute x0 -> x3, waiting for transfers between devices: none -> 26 us  [local(): lax.ppermute(ring[-1], 'vocab', [(dev, (dev + 1) % 4) for dev in range(4)])]
    all_gather x1 -> x0, waiting for transfers between devices: 23.7 us -> none  [local(): group_states = lax.all_gather(hidden, 'vocab', axis=0, tiled=True)]
    reduce_scatter x1, waiting for transfers between devices: 22.1 us -> 31.6 us  [local(): lax.psum_scatter(partial_grad, 'vocab', scatter_dimension=0, tiled=True)]
    all_gather x1, blocking collectives: 6.01 us -> 13.6 us  [local(): lax.all_gather(valid_mask, 'vocab', axis=0, tiled=True)]
    unnamed x5 -> x9, local copies, waits for them, and re-layouts: 12.7 us -> 6.95 us
  transfers between devices with their start and end apart: 4 -> 6, of which waited for: 4 -> 5; matrix products, arithmetic and copies ran while one was open for 5% -> 5% of each run, Pallas kernels for 0% -> 0%
where the time goes in v1:
time: 386 us; the launch traced here: 385 us
  waiting for transfers between devices  289 us (75%)
  blocking collectives  45.5 us (12%)
  matrix products  26.2 us (7%)
  between operations  15.5 us (4%)
  local copies, waits for them, and re-layouts  8.04 us (2%)
    reduce_scatter x1, waiting for transfers between devices, local(): lax.psum_scatter(lax.dot_general(state_cols, delta_logit, (((0,), (0,)),...  190 us
    all_gather x1, waiting for transfers between devices, local(): lax.all_gather(head_weight, 'batch', axis=1, tiled=True)  40.3 us
    reduce_scatter x1, waiting for transfers between devices, local(): lax.psum_scatter(partial_grad, 'vocab', scatter_dimension=0, tiled=True)  31.6 us
    ppermute x3, waiting for transfers between devices, local(): lax.ppermute(ring[-1], 'vocab', [(dev, (dev + 1) % 4) for dev in range(4)])  26 us
    psum x1, blocking collectives, local(): loss_total = lax.psum(jnp.sum(token_loss), 'batch')  20.6 us
    all_gather x1, blocking collectives, local(): lax.all_gather(valid_mask, 'vocab', axis=0, tiled=True)  13.6 us
    dot_general x1, matrix products, local(): lax.dot_general(state_cols, delta_logit, (((0,), (0,)), ((), ())), prefer...  11 us
    dot_general x1, matrix products, local(): jnp.dot(delta_logit, lax.all_gather(head_weight, 'batch', axis=1, tiled=T...  8.19 us
  transfers between devices with their start and end apart: 6, of which 5 were waited for; matrix products, arithmetic and copies ran while one was open for 5% of the time, Pallas kernels for 0%

profile of v1, /device:TPU:0, one launch (start us, length us, event | category | flops | bytes accessed | tf_op | source)
XLA Modules:
  0.0 385.3 jit_solution(4640610476716631942)
XLA Ops:
  7.2 0.0 all-gather.4.cloned.1.call-start
  7.2 0.7 all-gather.4.cloned.1.call-update
  7.9 0.0 reduce-scatter.5.cloned.1.call-start
  7.9 0.5 collective-permute-start
  8.5 13.2 %collective-permute-done = bf16[128,3584]{1,0:T(8,128)(2,1)S(1)} collective-permute-done((bf16[128,3584]{1,0:T(8,128)(2,1)}, bf16[128,3584]{1,0:T(8,128)(2,1)S(1)}, u32[]{:S(2)}, u32[]{:S(2)}) %collective-permute-start) | collective-permute-done | bytes 917536 | tf_op jit(solution)/shard_map/ppermute | solution.py:23
  21.7 0.0 collective-permute-start.1
  21.7 12.8 %collective-permute-done.1 = bf16[128,3584]{1,0:T(8,128)(2,1)S(1)} collective-permute-done((bf16[128,3584]{1,0:T(8,128)(2,1)S(1)}, bf16[128,3584]{1,0:T(8,128)(2,1)S(1)}, u32[]{:S(2)}, u32[]{:S(2)}) %collective-permute-start.1) | collective-permute-done | bytes 917536 | tf_op jit(solution)/shard_map/ppermute | solution.py:23
  34.5 0.0 collective-permute-start.2
  34.5 13.6 %all-gather = s32[4,1,128]{2,1,0:T(1,128)S(1)} all-gather(s32[1,1,128]{2,1,0:T(1,128)} %bitcast.13), channel_id=1, replica_groups=mesh['batch'=8,'vocab'=4] {'vocab'}, dimensions={0}, use_global_device_ids=true | all-gather | bytes 2560 | tf_op jit(solution)/shard_map/all_gather | solution.py:19
  48.2 5.6 %all-gather.1 = s32[4,1,128]{2,1,0:T(1,128)S(1)} all-gather(s32[1,1,128]{2,1,0:T(1,128)} %bitcast.14), channel_id=1, replica_groups=mesh['batch'=8,'vocab'=4] {'vocab'}, dimensions={0}, use_global_device_ids=true | all-gather | bytes 2560 | tf_op jit(solution)/shard_map/all_gather | solution.py:18
  53.7 0.0 collective-permute-done.2
  53.7 1.0 constant_dynamic-update-slice_fusion.7
  54.7 1.0 constant_dynamic-update-slice_fusion.6
  55.7 1.0 constant_dynamic-update-slice_fusion.5
  56.7 0.0 copy-done
  56.7 1.0 constant_dynamic-update-slice_fusion.4
  57.7 1.0 constant_dynamic-update-slice_fusion.3
  58.7 1.0 constant_dynamic-update-slice_fusion.2
  59.7 1.0 constant_dynamic-update-slice_fusion.1
  60.7 1.1 constant_dynamic-update-slice_fusion
  61.8 40.3 %all-gather.4.cloned.1.call-done = bf16[768,3584]{0,1:T(8,128)(2,1)} async-done(((bf16[768,448]{0,1:T(8,128)(2,1)}), bf16[768,3584]{0,1:T(8,128)(2,1)}) %all-gather.4.cloned.1.call-update) | async-done | bytes 5505040 | tf_op jit(solution)/shard_map/all_gather | solution.py:38
  102.0 7.0 %select_reduce_fusion = (f32[512]{0:T(512)S(1)}, f32[512]{0:T(512)S(1)}, f32[512,768]{1,0:T(8,128)S(1)}) fusion(s32[512]{0:T(512)S(1)} %bitcast.10, bf16[768,3584]{0,1:T(8,128)(2,1)} %all-gather.4.cloned.1.call-done, bf16[1024,3584]{1,0:T(8,128)(2,1)} %constant_dynamic-update-slice_fusion, s32[]{:T(128)S(6)} %select_n.22), kind=kOutput, calls=%fused_computation.4 | convolution fusion | flops 2820930560 | bytes 10754052 | tf_op jit(solution)/shard_map/dot_general | solution.py:36
  109.1 5.7 %all-reduce = (f32[512]{0:T(512)S(1)}, f32[512]{0:T(512)S(1)}) all-reduce(f32[512]{0:T(512)S(1)} %get-tuple-element.4, f32[512]{0:T(512)S(1)} %get-tuple-element.3), channel_id=1, replica_groups=mesh['batch'=8,'vocab'=4] {'vocab'}, use_global_device_ids=true, to_apply=%region_1.2 | all-reduce | flops 1024 | bytes 8192 | tf_op jit(solution)/shard_map/psum | solution.py:45
  114.7 8.2 %fusion.8 = f32[512,3584]{1,0:T(8,128)} fusion(bf16[768,3584]{0,1:T(8,128)(2,1)} %all-gather.4.cloned.1.call-done, f32[512,768]{1,0:T(8,128)S(1)} %get-tuple-element.7, s32[512]{0:T(512)S(1)} %bitcast.11, f32[512]{0:T(512)S(1)} %get-tuple-element.5, f32[512]{0:T(512)S(1)} %bitcast.7), kind=kOutput, calls=%fused_computation.21 | convolution fusion | flops 2822504448 | bytes 14424064 | tf_op jit(solution)/shard_map/dot_general | solution.py:62
  122.9 0.0 reduce-scatter.5.cloned.1.call-update
  122.9 0.0 reduce-scatter.3.cloned.1.call-start
  123.0 11.0 %fusion = f32[3584,768]{1,0:T(8,128)} fusion(bf16[1024,3584]{1,0:T(8,128)(2,1)} %constant_dynamic-update-slice_fusion, s32[]{:T(128)S(6)} %select_n.22, f32[512,768]{1,0:T(8,128)S(1)} %get-tuple-element.7, s32[512]{0:T(512)S(1)} %bitcast.12, f32[512]{0:T(512)S(1)} %get-tuple-element.5, f32[512]{0:T(512)S(1)} %bitcast.8), kind=kOutput, calls=%fused_computation | convolution fusion | flops 2822504448 | bytes 16259076 | tf_op jit(solution)/shard_map/dot_general | solution.py:54
  134.0 0.0 reduce-scatter.3.cloned.1.call-update
  134.0 0.6 multiply_reduce_fusion
  134.6 20.6 %psum.23 = f32[]{:T(128)} all-reduce(f32[]{:T(128)} %multiply_reduce_fusion), channel_id=1, replica_groups=mesh['batch'=8,'vocab'=4] {'batch'}, use_global_device_ids=true, to_apply=%region_7.8 | all-reduce | flops 1 | bytes 8 | tf_op jit(solution)/shard_map/psum | solution.py:70
  155.9 31.6 %reduce-scatter.5.cloned.1.call-done = f32[128,3584]{1,0:T(8,128)} async-done(((f32[512,3584]{1,0:T(8,128)}), f32[128,3584]{1,0:T(8,128)}) %reduce-scatter.5.cloned.1.call-update) | async-done | bytes 1835024 | tf_op jit(solution)/shard_map/reduce_scatter | solution.py:67
  187.5 190.2 %reduce-scatter.3.cloned.1.call-done = f32[448,768]{1,0:T(8,128)} async-done(((f32[3584,768]{1,0:T(8,128)}), f32[448,768]{1,0:T(8,128)}) %reduce-scatter.3.cloned.1.call-update) | async-done | bytes 1376272 | tf_op jit(solution)/shard_map/reduce_scatter | solution.py:53
  (3 shorter events, 0.0 us)
Async XLA Ops:
  7.2 94.9 %all-gather.4.cloned.1.call-start = ((), (), s32[]{:S(2)}) async-start(), calls=%async_computation.2 | async-start | bytes 6193152 | tf_op jit(solution)/shard_map/all_gather | solution.py:38
  7.9 179.6 %reduce-scatter.5.cloned.1.call-start = ((), (), s32[]{:S(2)}) async-start(), calls=%async_computation.4 | async-start | bytes 9175040 | tf_op jit(solution)/shard_map/reduce_scatter | solution.py:67
  7.9 13.7 %collective-permute-start = (bf16[128,3584]{1,0:T(8,128)(2,1)}, bf16[128,3584]{1,0:T(8,128)(2,1)S(1)}, u32[]{:S(2)}, u32[]{:S(2)}) collective-permute-start(bf16[128,3584]{1,0:T(8,128)(2,1)} %param.4), channel_id=1, source_target_pairs={{0,1},{1,2},{2,3},{3,0},{4,5},{5,6},{6,7},{7,4},{8,9},{9,10},{10,1... | collective-permute-start | bytes 2752520 | tf_op jit(solution)/shard_map/ppermute | solution.py:23
  21.7 12.8 %collective-permute-start.1 = (bf16[128,3584]{1,0:T(8,128)(2,1)S(1)}, bf16[128,3584]{1,0:T(8,128)(2,1)S(1)}, u32[]{:S(2)}, u32[]{:S(2)}) collective-permute-start(bf16[128,3584]{1,0:T(8,128)(2,1)S(1)} %collective-permute-done), channel_id=1, source_target_pairs={{0,1},{1,2},{2,3},{3,0},{4,5},{5,6},{6,7},{7,4},{8,9},{9,10},{10,1... | collective-permute-start | bytes 2752520 | tf_op jit(solution)/shard_map/ppermute | solution.py:23
  34.5 19.2 %collective-permute-start.2 = (bf16[128,3584]{1,0:T(8,128)(2,1)S(1)}, bf16[128,3584]{1,0:T(8,128)(2,1)S(1)}, u32[]{:S(2)}, u32[]{:S(2)}) collective-permute-start(bf16[128,3584]{1,0:T(8,128)(2,1)S(1)} %collective-permute-done.1), channel_id=1, source_target_pairs={{0,1},{1,2},{2,3},{3,0},{4,5},{5,6},{6,7},{7,4},{8,9},{9,10},{10,1... | collective-permute-start | bytes 2752520 | tf_op jit(solution)/shard_map/ppermute | solution.py:23
  54.7 2.0 copy-start
  122.9 254.7 %reduce-scatter.3.cloned.1.call-start = ((), (), s32[]{:S(2)}) async-start(), calls=%async_computation.3 | async-start | bytes 12386304 | tf_op jit(solution)/shard_map/reduce_scatter | solution.py:53
Sparse Core Ops, SparseCore 0:
  10.2 91.8 all-gather.3
  123.1 64.3 reduce-scatter.4
  191.7 185.9 reduce-scatter.2
